TPU v7x, 8 devices: a whole 2x2x1 slice. The times are simulated.
8 devices in a mesh: dp: 1 (over z), ing: 2 (over y), grp: 4 (over x, core).
Axes of the slice: x: 2, y: 2, z: 1, core: 2. Of those that a mesh axis runs over, the one named last changes fastest.
Arguments:
- tokens: bfloat16 [1024, 2048], P(('dp', 'grp', 'ing'))
- expert_ids: int32 [1024, 2, 2], P(('dp', 'grp', 'ing'))
- gate_vals: float32 [1024, 2, 2], P(('dp', 'grp', 'ing'))
- w_one: bfloat16 [32, 2048, 1792], P(('grp', 'ing'))
- w_three: bfloat16 [32, 2048, 1792], P(('grp', 'ing'))
- w_two: bfloat16 [32, 1792, 2048], P(('grp', 'ing'))
Outputs:
- output: bfloat16 [1024, 2048], P(('dp', 'grp', 'ing'))
All inputs are finite; a program needn't handle non-finite values.
Results may differ from a plain program's by a relative error of at most 0.00159.
Values are sent between devices in bfloat16 or wider.
A program may use at most 1 GiB of HBM per device.

v0:
```python
import jax
import jax.numpy as jnp
from jax import lax
from jax.sharding import PartitionSpec as P


def solution(mesh):
    grp_size = mesh.shape['grp']
    ing_size = mesh.shape['ing']
    row_spec = P(('dp', 'grp', 'ing'))
    exp_spec = P(('grp', 'ing'))

    def local_fn(tokens, expert_ids, gate_vals, w_one, w_three, w_two):
        tok_count, d_model = tokens.shape
        m_groups = expert_ids.shape[1]
        per_group = expert_ids.shape[2]
        top_k = m_groups * per_group
        exp_local = w_one.shape[0]
        exp_group = exp_local * ing_size
        n_experts = exp_group * grp_size
        cap_group = (tok_count * m_groups + grp_size - 1) // grp_size
        cap_exp = (cap_group * per_group + exp_group - 1) // exp_group

        tok_grp = expert_ids[:, :, 0] // exp_group
        grp_sel = jnp.any(tok_grp[:, :, None] == jnp.arange(grp_size), axis=1)
        sel_int = grp_sel.astype(jnp.int32)
        grp_slot = jnp.cumsum(sel_int, axis=0) - sel_int
        src_mask = grp_sel[:, :, None] & (grp_slot[:, :, None] == jnp.arange(cap_group))
        src_hot = src_mask.astype(jnp.bfloat16)
        flat_ids = expert_ids.reshape(tok_count, top_k)
        flat_gate = gate_vals.reshape(tok_count, top_k)
        gate_dense = jnp.sum(jnp.where(flat_ids[:, :, None] == jnp.arange(n_experts), flat_gate[:, :, None], 0.0), axis=1)
        gate_dense = gate_dense.reshape(tok_count, grp_size, exp_group)
        x_send = jnp.einsum('trc,td->rcd', src_hot, tokens, preferred_element_type=jnp.float32).astype(jnp.bfloat16)
        g_send = jnp.einsum('trc,tre->rce', src_mask.astype(jnp.float32), gate_dense, precision=lax.Precision.HIGHEST, preferred_element_type=jnp.float32)
        x_recv = lax.all_to_all(x_send, 'grp', 0, 0, tiled=True)
        g_recv = lax.all_to_all(g_send, 'grp', 0, 0, tiled=True)

        chosen = g_recv != 0.0
        chosen_int = chosen.astype(jnp.int32)
        exp_slot = jnp.cumsum(chosen_int, axis=1) - chosen_int
        fwd_mask = chosen[..., None] & (exp_slot[..., None] == jnp.arange(cap_exp))
        fwd_mask = fwd_mask.reshape(grp_size, cap_group, ing_size, exp_local, cap_exp)
        x_fan = jnp.einsum('scjlq,scd->ljsqd', fwd_mask.astype(jnp.bfloat16), x_recv, preferred_element_type=jnp.float32).astype(jnp.bfloat16)
        x_exp = lax.all_to_all(x_fan, 'ing', 1, 1, tiled=True)

        exp_rows = x_exp.reshape(exp_local, ing_size * grp_size * cap_exp, d_model)
        h_one = jnp.einsum('lrd,ldf->lrf', exp_rows, w_one, preferred_element_type=jnp.float32)
        h_three = jnp.einsum('lrd,ldf->lrf', exp_rows, w_three, preferred_element_type=jnp.float32)
        act_bf = (jax.nn.silu(h_one) * h_three).astype(jnp.bfloat16)
        exp_out = jnp.einsum('lrf,lfd->lrd', act_bf, w_two, preferred_element_type=jnp.float32).astype(jnp.bfloat16)
        exp_out = exp_out.reshape(exp_local, ing_size, grp_size, cap_exp, d_model)

        x_back = lax.all_to_all(exp_out, 'ing', 1, 1, tiled=True)
        weights = fwd_mask.astype(jnp.float32) * g_recv.reshape(grp_size, cap_group, ing_size, exp_local)[..., None]
        grp_sum = jnp.einsum('scjlq,ljsqd->scd', weights, x_back, precision=lax.Precision.HIGHEST, preferred_element_type=jnp.float32).astype(jnp.bfloat16)
        y_back = lax.all_to_all(grp_sum, 'grp', 0, 0, tiled=True)
        return jnp.einsum('trc,rcd->td', src_hot, y_back, preferred_element_type=jnp.float32).astype(jnp.bfloat16)

    return jax.shard_map(local_fn, mesh=mesh, in_specs=(row_spec, row_spec, row_spec, exp_spec, exp_spec, exp_spec), out_specs=row_spec, check_vma=False)
```

profile of v0, /device:TPU:0, one launch (start us, length us, event | category | flops | bytes accessed | tf_op | source)
XLA Modules:
  0.0 147.3 jit_solution(13699469450720908396)
XLA Ops:
  0.0 0.0 copy-start
  0.0 0.7 and_select_fusion
  0.8 0.1 copy.37
  0.9 0.2 reduce_window_sum.22
  1.1 0.1 copy.39
  1.1 0.7 select_reduce_fusion
  1.9 0.2 fusion.24
  2.1 0.7 reshape.40
  2.8 4.6 %all-to-all-start = ((f32[4,1,512]{2,1,0:T(1,128)}), f32[4,1,512]{2,1,0:T(1,128)S(1)}, u32[]{:S(2)}, u32[]{:S(2)}) async-start(f32[4,1,512]{2,1,0:T(1,128)} %reshape.40), calls=%async_computation | async-start | bytes 16384 | tf_op jit(solution)/shard_map/all_to_all | solution.py:37
  7.4 0.0 copy-done
  7.4 1.4 convolution_convert_fusion.1
  8.8 2.2 %all-to-all-done = f32[4,1,512]{2,1,0:T(1,128)S(1)} async-done(((f32[4,1,512]{2,1,0:T(1,128)}), f32[4,1,512]{2,1,0:T(1,128)S(1)}, u32[]{:S(2)}, u32[]{:S(2)}) %all-to-all-start) | async-done | bytes 8224 | tf_op jit(solution)/shard_map/all_to_all | solution.py:37
  11.0 3.5 %all-to-all-start.1 = ((bf16[4,64,2048]{2,1,0:T(8,128)(2,1)}), bf16[4,64,2048]{2,1,0:T(8,128)(2,1)S(1)}, u32[]{:S(2)}, u32[]{:S(2)}) async-start(bf16[4,64,2048]{2,1,0:T(8,128)(2,1)} %convolution_convert_fusion.1), calls=%async_computation.1 | async-start | bytes 2097152 | tf_op jit(solution)/shard_map/all_to_all | solution.py:36
  14.5 0.5 broadcast.30
  15.0 0.7 reduce
  15.7 0.1 reshape.41
  15.8 0.1 copy.41
  15.9 0.1 reduce_window_sum.23
  16.0 0.1 copy.42
  16.1 0.1 fusion.5
  16.2 12.5 %all-to-all-done.1 = bf16[4,64,2048]{2,1,0:T(8,128)(2,1)S(1)} async-done(((bf16[4,64,2048]{2,1,0:T(8,128)(2,1)}), bf16[4,64,2048]{2,1,0:T(8,128)(2,1)S(1)}, u32[]{:S(2)}, u32[]{:S(2)}) %all-to-all-start.1) | async-done | bytes 1048608 | tf_op jit(solution)/shard_map/all_to_all | solution.py:36
  28.7 0.7 fusion.29
  29.4 0.3 convert_bitcast_fusion
  29.7 0.1 copy.46
  29.9 27.6 %all_to_all.25 = bf16[4,2,4,16,2048]{4,3,0,2,1:T(8,128)(2,1)S(1)} all-to-all(bf16[4,2,4,16,2048]{4,3,0,2,1:T(8,128)(2,1)S(1)} %copy.46), channel_id=1, replica_groups=mesh['dp'=1,'ing'=2,'grp'=4] {'ing'}, dimensions={1} | all-to-all | bytes 4194304 | tf_op jit(solution)/shard_map/all_to_all | solution.py:45
  57.5 0.1 copy.47
  57.6 15.2 %fusion.30 = f32[4,128,1792]{2,1,0:T(8,128)} fusion(bf16[4,128,2048]{2,1,0:T(8,128)(2,1)S(1)} %bitcast.43, bf16[4,2048,1792]{2,1,0:T(8,128)(2,1)} %param.9), kind=kOutput, calls=%fused_computation.39 | convolution fusion | flops 3758096384 | bytes 35127296 | tf_op jit(solution)/shard_map/lrd,ldf->lrf/dot_general | solution.py:48
  72.8 15.2 %multiply_convert_fusion = bf16[4,128,1792]{2,1,0:T(8,128)(2,1)S(1)} fusion(f32[4,128,1792]{2,1,0:T(8,128)} %fusion.30, bf16[4,128,2048]{2,1,0:T(8,128)(2,1)S(1)} %bitcast.44, bf16[4,2048,1792]{2,1,0:T(8,128)(2,1)} %param.10), kind=kOutput, calls=%fused_computation | convolution fusion | flops 3763601408 | bytes 36962304 | tf_op jit(solution)/shard_map/lrd,ldf->lrf/dot_general | solution.py:49
  88.0 13.5 %convolution_convert_fusion = bf16[4,128,2048]{2,1,0:T(8,128)(2,1)S(1)} fusion(bf16[4,128,1792]{2,1,0:T(8,128)(2,1)S(1)} %multiply_convert_fusion, bf16[4,1792,2048]{2,1,0:T(8,128)(2,1)} %param.11), kind=kOutput, calls=%fused_computation.1 | convolution fusion | flops 3759144960 | bytes 33292288 | tf_op jit(solution)/shard_map/lrf,lfd->lrd/dot_general | solution.py:51
  101.5 0.2 copy.48
  101.8 0.0 copy-start.1
  101.8 26.4 %all_to_all.26 = bf16[4,2,4,16,2048]{4,3,2,0,1:T(8,128)(2,1)S(1)} all-to-all(bf16[4,2,4,16,2048]{4,3,2,0,1:T(8,128)(2,1)S(1)} %copy.48), channel_id=1, replica_groups=mesh['dp'=1,'ing'=2,'grp'=4] {'ing'}, dimensions={1} | all-to-all | bytes 4194304 | tf_op jit(solution)/shard_map/all_to_all | solution.py:54
  128.2 1.1 fusion
  129.3 16.9 %all_to_all.27 = bf16[4,64,2048]{2,1,0:T(8,128)(2,1)S(1)} all-to-all(bf16[4,64,2048]{2,1,0:T(8,128)(2,1)S(1)} %fusion), channel_id=1, replica_groups=mesh['dp'=1,'ing'=2,'grp'=4] {'grp'}, dimensions={0} | all-to-all | bytes 2097152 | tf_op jit(solution)/shard_map/all_to_all | solution.py:57
  146.1 1.1 fusion.1
  147.3 0.0 copy-done.1
  (6 shorter events, 0.1 us)
Async XLA Ops:
  0.0 7.4 %copy-start = (bf16[128,2048]{1,0:T(8,128)(2,1)S(1)}, bf16[128,2048]{1,0:T(8,128)(2,1)}, u32[]{:S(2)}) copy-start(bf16[128,2048]{1,0:T(8,128)(2,1)} %param.6) | copy-start | bytes 1572868
  2.8 8.2 %all-to-all-start = ((f32[4,1,512]{2,1,0:T(1,128)}), f32[4,1,512]{2,1,0:T(1,128)S(1)}, u32[]{:S(2)}, u32[]{:S(2)}) async-start(f32[4,1,512]{2,1,0:T(1,128)} %reshape.40), calls=%async_computation | async-start | bytes 16384 | tf_op jit(solution)/shard_map/all_to_all | solution.py:37
  11.0 17.7 %all-to-all-start.1 = ((bf16[4,64,2048]{2,1,0:T(8,128)(2,1)}), bf16[4,64,2048]{2,1,0:T(8,128)(2,1)S(1)}, u32[]{:S(2)}, u32[]{:S(2)}) async-start(bf16[4,64,2048]{2,1,0:T(8,128)(2,1)} %convolution_convert_fusion.1), calls=%async_computation.1 | async-start | bytes 2097152 | tf_op jit(solution)/shard_map/all_to_all | solution.py:36
  101.8 45.5 %copy-start.1 = (bf16[128,2048]{1,0:T(8,128)(2,1)S(1)}, bf16[128,2048]{1,0:T(8,128)(2,1)}, u32[]{:S(2)}) copy-start(bf16[128,2048]{1,0:T(8,128)(2,1)} %param.6) | copy-start | bytes 1572868
where the time goes:
time: 148 us; the launch traced here: 147 us
  blocking collectives  70.9 us (48%)
  matrix products  48.4 us (33%)
  waiting for transfers between devices  14.7 us (10%)
  starting transfers between devices  8.13 us (5%)
  other arithmetic  2.91 us (2%)
  local copies, waits for them, and re-layouts  2.17 us (1%)
    all_to_all x1, blocking collectives, local_fn(): x_exp = lax.all_to_all(x_fan, 'ing', 1, 1, tiled=True)  27.6 us
    all_to_all x1, blocking collectives, local_fn(): x_back = lax.all_to_all(exp_out, 'ing', 1, 1, tiled=True)  26.4 us
    all_to_all x1, blocking collectives, local_fn(): y_back = lax.all_to_all(grp_sum, 'grp', 0, 0, tiled=True)  16.9 us
    dot_general x1, matrix products, local_fn(): jnp.einsum('lrd,ldf->lrf', exp_rows, w_three, preferred_element_type=jnp....  15.2 us
    dot_general x1, matrix products, local_fn(): jnp.einsum('lrd,ldf->lrf', exp_rows, w_one, preferred_element_type=jnp.fl...  15.2 us
    dot_general x1, matrix products, local_fn(): jnp.einsum('lrf,lfd->lrd', act_bf, w_two, preferred_element_type=jnp.floa...  13.5 us
    all_to_all x1, waiting for transfers between devices, local_fn(): x_recv = lax.all_to_all(x_send, 'grp', 0, 0, tiled=True)  12.5 us
    all_to_all x1, starting transfers between devices, local_fn(): g_recv = lax.all_to_all(g_send, 'grp', 0, 0, tiled=True)  4.61 us
  transfers between devices with their start and end apart: 2, of which 2 were waited for; matrix products, arithmetic and copies ran while one was open for 2% of the time, Pallas kernels for 0%

commit v1 on v0

v1 whole, which is shorter than its diff:
```python
import functools

import jax
import jax.numpy as jnp
from jax import lax
from jax.experimental import pallas as pl
from jax.experimental.pallas import tpu as pltpu
from jax.sharding import PartitionSpec as P

MESH = pl.DeviceIdType.MESH
BF16 = jnp.bfloat16
F32 = jnp.float32
I32 = jnp.int32

TOK = 128
D = 2048
FF = 1792
EL = 4
CAP = 16
FC = 256
NF = FF // FC
NC = 512
N4 = D // NC
NB = 256
N8 = D // NB
NS = 22
CH = 4
CR = TOK // CH

BLOCK = {(1, 0, 0): 0, (1, 1, 0): 1, (1, 0, 1): 2, (1, 1, 1): 3,
         (0, 0, 0): 4, (0, 0, 1): 5, (0, 1, 0): 6, (0, 1, 1): 7}
PEERS = [(dy, dx, dc) for dy in (0, 1) for dx in (0, 1) for dc in (0, 1)][1:]
RET = [(0, 32, 1, 0, 0), (32, 32, 1, 1, 0), (80, 16, 0, 1, 0), (112, 16, 0, 1, 16)]


def kernel(ids_ref, gate_ref, tok_hbm, w1, w3, w2, y_ref,
           ring, T, X, act, E, R, PX, Q, PS, CM, GB, GH, META,
           ws_a, ws_b, tsem, bs, br, ss, sr, ms, mr, es, er, ps, pr):
    g = lax.axis_index('grp')
    y = lax.axis_index('ing')
    x = g // 2
    c = g % 2

    def peer(dy, dx, dc):
        return {'ing': (y + dy) % 2, 'grp': ((x + dx) % 2) * 2 + (c + dc) % 2}

    def remote(src, dst, s, r, to):
        return pltpu.make_async_remote_copy(src_ref=src, dst_ref=dst, send_sem=s, recv_sem=r, device_id=peer(*to), device_id_type=MESH)

    def w13(e, f, slot):
        col = pl.ds(pl.multiple_of(f * FC, FC), FC)
        return (pltpu.make_async_copy(w1.at[e, :, col], ring.at[slot, :, pl.ds(0, FC)], ws_a.at[slot]),
                pltpu.make_async_copy(w3.at[e, :, col], ring.at[slot, :, pl.ds(FC, FC)], ws_b.at[slot]))

    def w2c(e, n, slot):
        return (pltpu.make_async_copy(w2.at[e, :, pl.ds(n * NC, NC)], ring.at[slot, pl.ds(0, FF), :], ws_a.at[slot]),)

    def start(copies):
        for cp in copies:
            cp.start()

    def wait(copies):
        for cp in copies:
            cp.wait()

    own = pltpu.make_async_copy(tok_hbm, T.at[0, pl.ds(0, TOK), :], tsem)
    own.start()
    for e in (0, 1):
        for f in range(NF):
            start(w13(e, f, e * 11 + f))
        for n in range(N4):
            start(w2c(e, n, e * 11 + NF + n))

    META[0] = jnp.concatenate([ids_ref[...].astype(F32), gate_ref[...]], axis=0)

    barrier = pltpu.get_barrier_semaphore()
    for p in PEERS:
        pl.semaphore_signal(barrier, inc=1, device_id=peer(*p), device_id_type=MESH)
    pl.semaphore_wait(barrier, len(PEERS))

    metas = [remote(META.at[0], META.at[(p[0] * 2 + p[1]) * 2 + p[2]], ms.at[i], mr.at[i], p) for i, p in enumerate(PEERS)]
    start(metas)
    own.wait()

    def rows(k):
        return pl.ds(k * CR, CR)

    def rows2(k):
        return pl.ds(TOK + k * CR, CR)

    own_y = [remote(T.at[0, rows(k)], T.at[2, rows(k)], bs.at[0, k], br.at[0, k], (1, 0, 0)) for k in range(CH)]
    own_x = [remote(T.at[0, rows(k)], T.at[1, rows(k)], bs.at[1, k], br.at[1, k], (0, 1, 0)) for k in range(CH)]
    own_s = remote(T.at[0, pl.ds(0, TOK)], T.at[0, pl.ds(TOK, TOK)], ss.at[0], sr.at[0], (0, 0, 1))
    fwd = [remote(T.at[2 if k < CH // 2 else 1, rows(k)], T.at[3, rows(k)], bs.at[2, k], br.at[2, k],
                  (0, 1, 0) if k < CH // 2 else (1, 0, 0)) for k in range(CH)]
    y_s = [remote(T.at[2, rows(k)], T.at[2, rows2(k)], bs.at[3, k], br.at[3, k], (0, 0, 1)) for k in range(CH)]
    x_s = [remote(T.at[1, rows(k)], T.at[1, rows2(k)], bs.at[4, k], br.at[4, k], (0, 0, 1)) for k in range(CH)]
    d_s = [remote(T.at[3, rows(k)], T.at[3, rows2(k)], bs.at[5, k], br.at[5, k], (0, 0, 1)) for k in range(CH)]
    for k in range(CH):
        own_y[k].start()
        own_x[k].start()
    own_s.start()

    for m in metas:
        m.wait_recv()
    sub = lax.broadcasted_iota(I32, (TOK, TOK), 0)
    lane = lax.broadcasted_iota(I32, (TOK, TOK), 1)
    base = ((g * 2 + y) * EL).astype(F32)
    hot_rows = []
    for h in range(8):
        ids_h = META[h][0:4, :]
        for e in range(EL):
            hot_rows.append(jnp.sum(jnp.where(ids_h == base + e, 1.0, 0.0), axis=0, keepdims=True))
    hot = jnp.concatenate(hot_rows, axis=0)
    rank = jnp.dot(hot.astype(BF16), (sub < lane).astype(BF16), preferred_element_type=F32)
    key = jnp.where(hot > 0.0, rank, -1.0)
    slot16 = lax.broadcasted_iota(I32, (CAP, TOK), 0).astype(F32)
    zero16 = jnp.zeros((CAP, TOK), F32)
    for q in range(4):
        parts = []
        for e in range(EL):
            for dc in range(2):
                r = (q * 2 + dc) * EL + e
                hit = jnp.where(key[r:r + 1, :] == slot16, 1.0, 0.0)
                parts.append(jnp.concatenate([hit, zero16] if dc == 0 else [zero16, hit], axis=1))
        GH[q] = jnp.concatenate(parts, axis=0).astype(BF16)

    lower = (lane < sub).astype(BF16)
    lane_f = lane.astype(F32)
    col256 = lax.broadcasted_iota(I32, (TOK, 256), 1)
    for dx in range(2):
        meta_t = jnp.transpose(jnp.concatenate([META[dx * 2], jnp.zeros((TOK - 8, TOK), F32)], axis=0))
        ids_c = [meta_t[:, k:k + 1] for k in range(4)]
        gate_c = [meta_t[:, 4 + k:5 + k] for k in range(4)]
        hot_t = sum(jnp.where(ids_c[k] == lane_f, 1.0, 0.0) for k in range(4))
        rank_t = jnp.dot(lower, hot_t.astype(BF16), preferred_element_type=F32)
        row_of, dc_of = [], []
        for k in range(4):
            slot = jnp.sum(jnp.where(ids_c[k] == lane_f, rank_t, 0.0), axis=1, keepdims=True).astype(I32)
            idi = ids_c[k].astype(I32)
            dcr = ((idi >> 3) + c) & 1
            dyr = ((idi >> 2) + y) & 1
            row_of.append(dyr * 128 + (idi & 3) * 32 + dx * 16 + slot)
            dc_of.append(jnp.where((idi >> 4) == x, dcr, 2))
        for dc in range(2):
            for u in range(2):
                sel = [dc_of[2 * m + u] == dc for m in range(2)]
                row = jnp.where(sel[0], row_of[u], jnp.where(sel[1], row_of[2 + u], -1))
                gate = jnp.where(sel[0], gate_c[u], jnp.where(sel[1], gate_c[2 + u], 0.0))
                CM[dc, pl.ds((dx * 2 + u) * TOK, TOK), :] = jnp.where(row == col256, 1.0, 0.0).astype(BF16)
                GB[(dc * 2 + dx) * 2 + u] = jnp.broadcast_to(gate, (TOK, TOK))

    def gather(q):
        dy, dx = q // 2, q % 2
        for n in range(N4):
            cols = pl.ds(n * NC, NC)
            got = jnp.dot(GH[q], T[q, :, cols], preferred_element_type=F32).astype(BF16)
            for e in range(EL):
                for dc in range(2):
                    i = (e * 2 + dc) * CAP
                    X[e, pl.ds(BLOCK[(dy, dx, dc)] * CAP, CAP), cols] = got[i:i + CAP, :]

    for k in range(CH):
        own_y[k].wait_recv()
        y_s[k].start()
        if k < CH // 2:
            fwd[k].start()
        own_x[k].wait_recv()
        x_s[k].start()
        if k >= CH // 2:
            fwd[k].start()
    own_s.wait_recv()
    gather(0)
    for k in range(CH):
        y_s[k].wait_recv()
        x_s[k].wait_recv()
    gather(1)
    gather(2)
    for k in range(CH):
        fwd[k].wait_recv()
        d_s[k].start()
    for k in range(CH):
        d_s[k].wait_recv()
    gather(3)

    def layer1(e, a, f_lo, f_hi, base_slot, after):
        def body(f, carry):
            slot = base_slot + f
            wait(w13(e, f, slot))
            h = jnp.dot(X[e], ring[slot], preferred_element_type=F32)
            h1 = h[:, :FC]
            act[a, :, pl.ds(pl.multiple_of(f * FC, FC), FC)] = (jax.nn.silu(h1) * h[:, FC:]).astype(BF16)
            if after is not None:
                after(f)
            return carry
        lax.fori_loop(f_lo, f_hi, body, 0)

    def layer2(e, a, n, slot):
        wait(w2c(e, n, slot))
        out = jnp.dot(act[a], ring[slot, pl.ds(0, FF), :], preferred_element_type=F32).astype(BF16)
        for i in range(2):
            blk = out[:, i * NB:(i + 1) * NB]
            E[2 * n + i, e] = blk
            R[2 * n + i, 0, 0, e, pl.ds(0, CAP), :] = blk[64:80, :]
            R[2 * n + i, 0, 0, e, pl.ds(CAP, CAP), :] = blk[96:112, :]

    sends = []

    def send(n0, nn, e0, ne, grp):
        for i, (r0, nr, dy, dc, d0) in enumerate(RET):
            cp = remote(E.at[pl.ds(n0, nn), pl.ds(e0, ne), pl.ds(r0, nr), :],
                        R.at[pl.ds(n0, nn), dc, dy, pl.ds(e0, ne), pl.ds(d0, nr), :],
                        es.at[i, grp], er.at[i, grp], (dy, 0, dc))
            cp.start()
            sends.append(cp)

    layer1(0, 0, 0, NF, 0, lambda f: start(w13(2, f, f)))
    for n in range(N4):
        layer2(0, 0, n, NF + n)
        start(w13(3, n, NF + n))
        if n % 2 == 1:
            send(2 * n - 2, 4, 0, 1, n // 2)
    layer1(1, 0, 0, 3, 11, lambda f: start(w13(3, f + 4, 11 + f)))
    for f in range(3, NF):
        layer1(1, 0, f, f + 1, 11, None)
        start(w2c(2 + (f - 3) % 2, (f - 3) // 2, 11 + f))
    for n in range(N4):
        layer2(1, 0, n, 18 + n)
        start(w2c(2 + n % 2, 2 + n // 2, 18 + n))
        if n % 2 == 1:
            send(2 * n - 2, 4, 1, 1, 2 + n // 2)
    layer1(2, 0, 0, NF, 0, None)
    layer1(3, 1, 0, NF, 7, None)
    for n in range(N4):
        for e in (2, 3):
            layer2(e, e - 2, n, 14 + 2 * n + e - 2)
        for i in range(2):
            send(2 * n + i, 1, 2, 2, 4 + 2 * n + i)

    gone = [remote(PX.at[n], Q.at[n], ps.at[n], pr.at[n], (0, 1, 0)) for n in range(N8)]

    def finish(n):
        gone[n].wait_recv()
        y_ref[:, pl.ds(n * NB, NB)] = (PS[n].astype(F32) + Q[n].astype(F32)).astype(BF16)

    for n in range(N8):
        if n % 4 == 0:
            for cp in sends[4 * (n // 4):4 * (n // 4) + 4] + sends[8 + 4 * (n // 4):8 + 4 * (n // 4) + 4]:
                cp.wait_recv()
        for cp in sends[16 + 4 * n:16 + 4 * n + 4]:
            cp.wait_recv()
        rows_n = [R[n, dc].reshape(256, NB) for dc in range(2)]
        for dx in (1, 0):
            total = jnp.zeros((TOK, NB), F32)
            for dc in range(2):
                part = jnp.dot(CM[dc, pl.ds(dx * 2 * TOK, 2 * TOK), :], rows_n[dc], preferred_element_type=F32)
                g0 = GB[(dc * 2 + dx) * 2]
                g1 = GB[(dc * 2 + dx) * 2 + 1]
                g0 = jnp.concatenate([g0, g0], axis=1)
                g1 = jnp.concatenate([g1, g1], axis=1)
                total = total + (g0 * part[:TOK] + g1 * part[TOK:]).astype(BF16).astype(F32)
            if dx == 1:
                PX[n] = total.astype(BF16)
                gone[n].start()
            else:
                PS[n] = total.astype(BF16)
        if n >= 2:
            finish(n - 2)
    finish(N8 - 2)
    finish(N8 - 1)

    for cp in metas + own_y + own_x + [own_s] + fwd + y_s + x_s + d_s + sends + gone:
        cp.wait_send()


def solution(mesh):
    row_spec = P(('dp', 'grp', 'ing'))
    exp_spec = P(('grp', 'ing'))

    def local_fn(tokens, expert_ids, gate_vals, w_one, w_three, w_two):
        ids = expert_ids.reshape(TOK, 4).T
        gates = gate_vals.reshape(TOK, 4).T
        dma = pltpu.SemaphoreType.DMA
        anywhere = pl.BlockSpec(memory_space=pl.ANY)
        vmem = pl.BlockSpec(memory_space=pltpu.VMEM)
        return pl.pallas_call(
            kernel,
            out_shape=jax.ShapeDtypeStruct((TOK, D), BF16),
            in_specs=[vmem, vmem, anywhere, anywhere, anywhere, anywhere],
            out_specs=vmem,
            scratch_shapes=[
                pltpu.VMEM((NS, D, 2 * FC), BF16),
                pltpu.VMEM((4, 2 * TOK, D), BF16),
                pltpu.VMEM((EL, 8 * CAP, D), BF16),
                pltpu.VMEM((2, 8 * CAP, FF), BF16),
                pltpu.VMEM((N8, EL, 8 * CAP, NB), BF16),
                pltpu.VMEM((N8, 2, 2, EL, 2 * CAP, NB), BF16),
                pltpu.VMEM((N8, TOK, NB), BF16),
                pltpu.VMEM((N8, TOK, NB), BF16),
                pltpu.VMEM((N8, TOK, NB), BF16),
                pltpu.VMEM((2, 4 * TOK, 256), BF16),
                pltpu.VMEM((8, TOK, TOK), F32),
                pltpu.VMEM((4, 128, 256), BF16),
                pltpu.VMEM((8, 8, TOK), F32),
                dma((NS,)), dma((NS,)), dma(()),
                dma((6, CH)), dma((6, CH)), dma((1,)), dma((1,)),
                dma((7,)), dma((7,)),
                dma((4, 12)), dma((4, 12)), dma((N8,)), dma((N8,)),
            ],
            compiler_params=pltpu.CompilerParams(collective_id=0, has_side_effects=True, vmem_limit_bytes=67043328),
        )(ids, gates, tokens, w_one, w_three, w_two)

    return jax.shard_map(local_fn, mesh=mesh, in_specs=(row_spec, row_spec, row_spec, exp_spec, exp_spec, exp_spec), out_specs=row_spec, check_vma=False)
```

time: 148 us -> 76.4 us (0.52)
  Pallas kernels: 0 us -> 74.3 us
  blocking collectives: 70.9 us -> 0 us
  matrix products: 48.4 us -> 0 us
  waiting for transfers between devices: 14.7 us -> 0 us
  starting transfers between devices: 8.13 us -> 0 us
  other arithmetic: 2.91 us -> 0 us
    pallas_call x0 -> x1, Pallas kernels: none -> 74.3 us  [local_fn(): pl.pallas_call(kernel, out_shape=jax.ShapeDtypeStruct((TOK, D), BF16), in...]
    all_to_all x3 -> x0, blocking collectives: 70.9 us -> none  [the longest x1 27.6 us: local_fn(): x_exp = lax.all_to_all(x_fan, 'ing', 1, 1, tiled=True)]
    dot_general x7 -> x0, matrix products: 47.7 us -> none  [the longest x1 15.2 us: local_fn(): jnp.einsum('lrd,ldf->lrf', exp_rows, w_three, preferred_element_type=jnp....]
    all_to_all x2 -> x0, waiting for transfers between devices: 14.7 us -> none  [the longest x1 12.5 us: local_fn(): x_recv = lax.all_to_all(x_send, 'grp', 0, 0, tiled=True)]
    all_to_all x2 -> x0, starting transfers between devices: 8.13 us -> none  [the longest x1 4.61 us: local_fn(): g_recv = lax.all_to_all(g_send, 'grp', 0, 0, tiled=True)]
  transfers between devices with their start and end apart: 2 -> 0, of which waited for: 2 -> 0; matrix products, arithmetic and copies ran while one was open for 2% -> 0% of each run, Pallas kernels for 0% -> 0%
where the time goes in v1:
time: 76.4 us; the launch traced here: 76.2 us
  Pallas kernels  74.3 us (97%)
  local copies, waits for them, and re-layouts  1.88 us (2%)
    pallas_call x1, Pallas kernels, local_fn(): pl.pallas_call(kernel, out_shape=jax.ShapeDtypeStruct((TOK, D), BF16), in...  74.3 us
    unnamed x1, local copies, waits for them, and re-layouts  1.88 us

profile of v1, /device:TPU:0, one launch (start us, length us, event | category | flops | bytes accessed | tf_op | source)
XLA Modules:
  0.0 76.2 jit_solution(4298687466574949201)
XLA Ops:
  0.0 74.3 %shard_map.64 = bf16[128,2048]{1,0:T(8,128)(2,1)} custom-call(s32[4,128]{1,0:T(4,128)} %bitcast.6, f32[4,128]{1,0:T(4,128)} %bitcast.7, bf16[128,2048]{1,0:T(8,128)(2,1)} %tok_hbm.1, bf16[4,2048,1792]{2,1,0:T(8,128)(2,1)} %w1.1, bf16[4,2048,1792]{2,1,0:T(8,128)(2,1)} %w3.1, bf16[4,1792,2048]{2,1,0:T(8,128)(2,1)} %w2.1), custom_call_target="tpu_custom_call" | custom-call | tf_op jit(solution)/shard_map/pallas_call | solution.py:286
  74.3 1.9 %copy.8 = bf16[128,2048]{1,0:T(8,128)(2,1)} copy(bf16[128,2048]{1,0:T(8,128)(2,1)} %shard_map.64) | data formatting | bytes 1048576

commit v2 on v1

--- a/solution.py
+++ b/solution.py
@@ -57,7 +57,7 @@
 
     def start(copies):
         for cp in copies:
-            cp.start()
+            cp.start(priority=1)
 
     def wait(copies):
         for cp in copies:
@@ -79,7 +79,8 @@
     pl.semaphore_wait(barrier, len(PEERS))
 
     metas = [remote(META.at[0], META.at[(p[0] * 2 + p[1]) * 2 + p[2]], ms.at[i], mr.at[i], p) for i, p in enumerate(PEERS)]
-    start(metas)
+    for cp in metas:
+        cp.start()
     own.wait()
 
     def rows(k):
@@ -183,17 +184,11 @@
         d_s[k].wait_recv()
     gather(3)
 
-    def layer1(e, a, f_lo, f_hi, base_slot, after):
-        def body(f, carry):
-            slot = base_slot + f
-            wait(w13(e, f, slot))
-            h = jnp.dot(X[e], ring[slot], preferred_element_type=F32)
-            h1 = h[:, :FC]
-            act[a, :, pl.ds(pl.multiple_of(f * FC, FC), FC)] = (jax.nn.silu(h1) * h[:, FC:]).astype(BF16)
-            if after is not None:
-                after(f)
-            return carry
-        lax.fori_loop(f_lo, f_hi, body, 0)
+    def layer1(e, a, f, slot):
+        wait(w13(e, f, slot))
+        h = jnp.dot(X[e], ring[slot], preferred_element_type=F32)
+        h1 = h[:, :FC]
+        act[a, :, pl.ds(f * FC, FC)] = (jax.nn.silu(h1) * h[:, FC:]).astype(BF16)
 
     def layer2(e, a, n, slot):
         wait(w2c(e, n, slot))
@@ -205,6 +200,7 @@
             R[2 * n + i, 0, 0, e, pl.ds(CAP, CAP), :] = blk[96:112, :]
 
     sends = []
+    arrive = {}
 
     def send(n0, nn, e0, ne, grp):
         for i, (r0, nr, dy, dc, d0) in enumerate(RET):
@@ -213,29 +209,33 @@
                         es.at[i, grp], er.at[i, grp], (dy, 0, dc))
             cp.start()
             sends.append(cp)
-
-    layer1(0, 0, 0, NF, 0, lambda f: start(w13(2, f, f)))
+            arrive.setdefault(grp, []).append(cp)
+
+    for f in range(NF):
+        layer1(0, 0, f, f)
+        start(w13(2, f, f))
     for n in range(N4):
         layer2(0, 0, n, NF + n)
         start(w13(3, n, NF + n))
-        if n % 2 == 1:
-            send(2 * n - 2, 4, 0, 1, n // 2)
-    layer1(1, 0, 0, 3, 11, lambda f: start(w13(3, f + 4, 11 + f)))
-    for f in range(3, NF):
-        layer1(1, 0, f, f + 1, 11, None)
-        start(w2c(2 + (f - 3) % 2, (f - 3) // 2, 11 + f))
+        send(2 * n, 2, 0, 1, n)
+    for f in range(NF):
+        layer1(1, 1, f, 11 + f)
+        if f < 3:
+            start(w13(3, f + 4, 11 + f))
+        else:
+            start(w2c(2 + (f - 3) % 2, (f - 3) // 2, 11 + f))
     for n in range(N4):
-        layer2(1, 0, n, 18 + n)
+        layer2(1, 1, n, 18 + n)
         start(w2c(2 + n % 2, 2 + n // 2, 18 + n))
-        if n % 2 == 1:
-            send(2 * n - 2, 4, 1, 1, 2 + n // 2)
-    layer1(2, 0, 0, NF, 0, None)
-    layer1(3, 1, 0, NF, 7, None)
+        send(2 * n, 2, 1, 1, 4 + n)
+    for e in (2, 3):
+        for f in range(NF):
+            layer1(e, e - 2, f, (e - 2) * NF + f)
     for n in range(N4):
         for e in (2, 3):
             layer2(e, e - 2, n, 14 + 2 * n + e - 2)
         for i in range(2):
-            send(2 * n + i, 1, 2, 2, 4 + 2 * n + i)
+            send(2 * n + i, 1, 2, 2, 8 + 2 * n + i)
 
     gone = [remote(PX.at[n], Q.at[n], ps.at[n], pr.at[n], (0, 1, 0)) for n in range(N8)]
 
@@ -244,11 +244,9 @@
         y_ref[:, pl.ds(n * NB, NB)] = (PS[n].astype(F32) + Q[n].astype(F32)).astype(BF16)
 
     for n in range(N8):
-        if n % 4 == 0:
-            for cp in sends[4 * (n // 4):4 * (n // 4) + 4] + sends[8 + 4 * (n // 4):8 + 4 * (n // 4) + 4]:
+        for grp in ([n // 2, 4 + n // 2] if n % 2 == 0 else []) + [8 + n]:
+            for cp in arrive[grp]:
                 cp.wait_recv()
-        for cp in sends[16 + 4 * n:16 + 4 * n + 4]:
-            cp.wait_recv()
         rows_n = [R[n, dc].reshape(256, NB) for dc in range(2)]
         for dx in (1, 0):
             total = jnp.zeros((TOK, NB), F32)
@@ -305,7 +303,7 @@
                 dma((NS,)), dma((NS,)), dma(()),
                 dma((6, CH)), dma((6, CH)), dma((1,)), dma((1,)),
                 dma((7,)), dma((7,)),
-                dma((4, 12)), dma((4, 12)), dma((N8,)), dma((N8,)),
+                dma((4, 16)), dma((4, 16)), dma((N8,)), dma((N8,)),
             ],
             compiler_params=pltpu.CompilerParams(collective_id=0, has_side_effects=True, vmem_limit_bytes=67043328),
         )(ids, gates, tokens, w_one, w_three, w_two)

time: 76.4 us -> 64.8 us (0.85)
  Pallas kernels: 74.3 us -> 62.7 us
    pallas_call x1, Pallas kernels: 74.3 us -> 62.7 us  [local_fn(): pl.pallas_call(kernel, out_shape=jax.ShapeDtypeStruct((TOK, D), BF16), in...]
where the time goes in v2:
time: 64.8 us; the launch traced here: 64.6 us
  Pallas kernels  62.7 us (97%)
  local copies, waits for them, and re-layouts  1.88 us (3%)
    pallas_call x1, Pallas kernels, local_fn(): pl.pallas_call(kernel, out_shape=jax.ShapeDtypeStruct((TOK, D), BF16), in...  62.7 us
    unnamed x1, local copies, waits for them, and re-layouts  1.88 us

profile of v2, /device:TPU:0, one launch (start us, length us, event | category | flops | bytes accessed | tf_op | source)
XLA Modules:
  0.0 64.6 jit_solution(3805069227327336037)
XLA Ops:
  0.0 62.7 %shard_map.64 = bf16[128,2048]{1,0:T(8,128)(2,1)} custom-call(s32[4,128]{1,0:T(4,128)} %bitcast.6, f32[4,128]{1,0:T(4,128)} %bitcast.7, bf16[128,2048]{1,0:T(8,128)(2,1)} %tok_hbm.1, bf16[4,2048,1792]{2,1,0:T(8,128)(2,1)} %w1.1, bf16[4,2048,1792]{2,1,0:T(8,128)(2,1)} %w3.1, bf16[4,1792,2048]{2,1,0:T(8,128)(2,1)} %w2.1), custom_call_target="tpu_custom_call" | custom-call | tf_op jit(solution)/shard_map/pallas_call | solution.py:284
  62.7 1.9 %copy.8 = bf16[128,2048]{1,0:T(8,128)(2,1)} copy(bf16[128,2048]{1,0:T(8,128)(2,1)} %shard_map.64) | data formatting | bytes 1048576

commit v3 on v2

v3 whole, which is shorter than its diff:
```python
import functools

import jax
import jax.numpy as jnp
from jax import lax
from jax.experimental import pallas as pl
from jax.experimental.pallas import tpu as pltpu
from jax.sharding import PartitionSpec as P

MESH = pl.DeviceIdType.MESH
BF16 = jnp.bfloat16
F32 = jnp.float32
I32 = jnp.int32

TOK = 128
D = 2048
FF = 1792
EL = 4
CAP = 16
FC = 256
NF = FF // FC
NC = 512
N4 = D // NC
NB = 256
N8 = D // NB
CH = 4
CR = TOK // CH

NS = 24

BLOCK = {(1, 0, 0): 0, (1, 0, 1): 1, (0, 0, 0): 2, (0, 0, 1): 3,
         (0, 1, 0): 4, (0, 1, 1): 5, (1, 1, 0): 6, (1, 1, 1): 7}
NEAR = 6 * CAP
PEERS = [(dy, dx, dc) for dy in (0, 1) for dx in (0, 1) for dc in (0, 1)][1:]
RET = [(0, 1, 0, 0), (16, 1, 1, 0), (48, 0, 1, 0), (80, 0, 1, 16), (96, 1, 0, 16), (112, 1, 1, 16)]

FETCH = []
for _e in (1, 0):
    FETCH += [(1, _e, _f) for _f in range(NF)] + [(2, _e, _n) for _n in range(N4)]
for _e in (2, 3):
    FETCH += [(1, _e, _f) for _f in range(NF)]
for _n in range(N4):
    FETCH += [(2, _e, _n) for _e in (2, 3)]
ACT = {1: 0, 2: 1, 3: 2, 0: 2}


def kernel(ids_ref, gate_ref, tok_hbm, w1, w3, w2, y_hbm,
           ring, T, X, act, E, R, PX, Q, PS, CM, GB, GH, META,
           ws_a, ws_b, tsem, bs, br, ss, sr, ms, mr, es, er, ps, pr, ysem):
    g = lax.axis_index('grp')
    y = lax.axis_index('ing')
    x = g // 2
    c = g % 2

    def peer(dy, dx, dc):
        return {'ing': (y + dy) % 2, 'grp': ((x + dx) % 2) * 2 + (c + dc) % 2}

    def remote(src, dst, s, r, to):
        return pltpu.make_async_remote_copy(src_ref=src, dst_ref=dst, send_sem=s, recv_sem=r, device_id=peer(*to), device_id_type=MESH)

    def w13(e, f, slot):
        col = pl.ds(pl.multiple_of(f * FC, FC), FC)
        return (pltpu.make_async_copy(w1.at[e, :, col], ring.at[slot, :, pl.ds(0, FC)], ws_a.at[slot]),
                pltpu.make_async_copy(w3.at[e, :, col], ring.at[slot, :, pl.ds(FC, FC)], ws_b.at[slot]))

    def w2c(e, n, slot):
        return (pltpu.make_async_copy(w2.at[e, :, pl.ds(n * NC, NC)], ring.at[slot, pl.ds(0, FF), :], ws_a.at[slot]),)

    def start(copies):
        for cp in copies:
            cp.start(priority=1)

    def wait(copies):
        for cp in copies:
            cp.wait()

    own = pltpu.make_async_copy(tok_hbm, T.at[0, pl.ds(0, TOK), :], tsem)
    own.start()
    slot_of = {}
    queue = list(FETCH)

    def fetch(chunk):
        layer, e, j = chunk
        return (w13 if layer == 1 else w2c)(e, j, slot_of[chunk])

    def refill(slot):
        if queue:
            chunk = queue.pop(0)
            slot_of[chunk] = slot
            start(fetch(chunk))

    for i in range(NS):
        refill(i)

    META[0] = jnp.concatenate([ids_ref[...].astype(F32), gate_ref[...]], axis=0)

    barrier = pltpu.get_barrier_semaphore()
    direct = [(0, 0, 1), (0, 1, 0), (1, 0, 0), (1, 0, 1)]
    for p in direct:
        pl.semaphore_signal(barrier, inc=1, device_id=peer(*p), device_id_type=MESH)
    pl.semaphore_wait(barrier, len(direct))

    metas = [remote(META.at[i], META.at[j], ms.at[k], mr.at[k], to) for k, (i, j, to) in enumerate([
        (0, 4, (1, 0, 0)), (0, 2, (0, 1, 0)), (0, 1, (0, 0, 1)),
        (4, 5, (0, 0, 1)), (4, 6, (0, 1, 0)), (2, 3, (0, 0, 1)), (6, 7, (0, 0, 1))])]
    for m in metas[:3]:
        m.start()
    own.wait()

    def rows(k):
        return pl.ds(k * CR, CR)

    def rows2(k):
        return pl.ds(TOK + k * CR, CR)

    own_y = [remote(T.at[0, rows(k)], T.at[2, rows(k)], bs.at[0, k], br.at[0, k], (1, 0, 0)) for k in range(CH)]
    own_x = [remote(T.at[0, rows(k)], T.at[1, rows(k)], bs.at[1, k], br.at[1, k], (0, 1, 0)) for k in range(CH)]
    own_s = remote(T.at[0, pl.ds(0, TOK)], T.at[0, pl.ds(TOK, TOK)], ss.at[0], sr.at[0], (0, 0, 1))
    fwd = [remote(T.at[2 if k < CH // 2 else 1, rows(k)], T.at[3, rows(k)], bs.at[2, k], br.at[2, k],
                  (0, 1, 0) if k < CH // 2 else (1, 0, 0)) for k in range(CH)]
    y_s = [remote(T.at[2, rows(k)], T.at[2, rows2(k)], bs.at[3, k], br.at[3, k], (0, 0, 1)) for k in range(CH)]
    x_s = [remote(T.at[1, rows(k)], T.at[1, rows2(k)], bs.at[4, k], br.at[4, k], (0, 0, 1)) for k in range(CH)]
    d_s = [remote(T.at[3, rows(k)], T.at[3, rows2(k)], bs.at[5, k], br.at[5, k], (0, 0, 1)) for k in range(CH)]
    own_y[0].start()
    own_x[0].start()
    metas[0].wait_recv()
    metas[4].start()
    metas[3].start()
    metas[1].wait_recv()
    metas[5].start()
    for k in range(1, CH):
        own_y[k].start()
        own_x[k].start()
    own_s.start()

    metas[4].wait_recv()
    metas[6].start()
    for i in (2, 3, 5, 6):
        metas[i].wait_recv()
    sub = lax.broadcasted_iota(I32, (TOK, TOK), 0)
    lane = lax.broadcasted_iota(I32, (TOK, TOK), 1)
    base = ((g * 2 + y) * EL).astype(F32)
    hot_rows = []
    for h in range(8):
        ids_h = META[h][0:4, :]
        for e in range(EL):
            hot_rows.append(jnp.sum(jnp.where(ids_h == base + e, 1.0, 0.0), axis=0, keepdims=True))
    hot = jnp.concatenate(hot_rows, axis=0)
    rank = jnp.dot(hot.astype(BF16), (sub < lane).astype(BF16), preferred_element_type=F32)
    key = jnp.where(hot > 0.0, rank, -1.0)
    slot16 = lax.broadcasted_iota(I32, (CAP, TOK), 0).astype(F32)
    zero16 = jnp.zeros((CAP, TOK), F32)
    for q in range(4):
        parts = []
        for e in range(EL):
            for dc in range(2):
                r = (q * 2 + dc) * EL + e
                hit = jnp.where(key[r:r + 1, :] == slot16, 1.0, 0.0)
                parts.append(jnp.concatenate([hit, zero16] if dc == 0 else [zero16, hit], axis=1))
        GH[q] = jnp.concatenate(parts, axis=0).astype(BF16)

    lower = (lane < sub).astype(BF16)
    lane_f = lane.astype(F32)
    for dx in range(2):
        meta_t = jnp.transpose(jnp.concatenate([META[dx * 2], jnp.zeros((TOK - 8, TOK), F32)], axis=0))
        ids_c = [meta_t[:, k:k + 1] for k in range(4)]
        gate_c = [meta_t[:, 4 + k:5 + k] for k in range(4)]
        hot_t = sum(jnp.where(ids_c[k] == lane_f, 1.0, 0.0) for k in range(4))
        rank_t = jnp.dot(lower, hot_t.astype(BF16), preferred_element_type=F32)
        row_of, dc_of = [], []
        for k in range(4):
            slot = jnp.sum(jnp.where(ids_c[k] == lane_f, rank_t, 0.0), axis=1, keepdims=True).astype(I32)
            idi = ids_c[k].astype(I32)
            dcr = ((idi >> 3) + c) & 1
            dyr = ((idi >> 2) + y) & 1
            row_of.append(dyr * 64 + (idi & 3) * CAP + slot)
            dc_of.append(jnp.where((idi >> 4) == x, dcr, 2))
        for dc in range(2):
            for u in range(2):
                sel = [dc_of[2 * m + u] == dc for m in range(2)]
                row = jnp.where(sel[0], row_of[u], jnp.where(sel[1], row_of[2 + u], -1))
                gate = jnp.where(sel[0], gate_c[u], jnp.where(sel[1], gate_c[2 + u], 0.0))
                CM[dc, pl.ds((dx * 2 + u) * TOK, TOK), :] = jnp.where(row == lane, 1.0, 0.0).astype(BF16)
                GB[(dc * 2 + dx) * 2 + u] = jnp.broadcast_to(gate, (TOK, TOK))

    def gather(q):
        dy, dx = q // 2, q % 2
        for n in range(N4):
            cols = pl.ds(n * NC, NC)
            got = jnp.dot(GH[q], T[q, :, cols], preferred_element_type=F32).astype(BF16)
            for e in range(EL):
                for dc in range(2):
                    i = (e * 2 + dc) * CAP
                    X[e, pl.ds(BLOCK[(dy, dx, dc)] * CAP, CAP), cols] = got[i:i + CAP, :]

    def far(k):
        fwd[k].wait_recv()
        d_s[k].start()

    for k in range(CH):
        own_y[k].wait_recv()
        y_s[k].start()
        if k < CH // 2:
            fwd[k].start()
        own_x[k].wait_recv()
        x_s[k].start()
        if k >= CH // 2:
            fwd[k].start()
    own_s.wait_recv()
    gather(0)
    for k in range(CH):
        y_s[k].wait_recv()
        x_s[k].wait_recv()
    gather(1)
    gather(2)

    waited = set()

    def layer1(chunk, r0, r1):
        _, e, f = chunk
        h = jnp.dot(X[e, r0:r1, :], ring[slot_of[chunk]], preferred_element_type=F32)
        h1 = h[:, :FC]
        act[ACT[e], r0:r1, f * FC:(f + 1) * FC] = (jax.nn.silu(h1) * h[:, FC:]).astype(BF16)

    def layer2(chunk, r0, r1):
        _, e, n = chunk
        out = jnp.dot(act[ACT[e], r0:r1, :], ring[slot_of[chunk], 0:FF, :], preferred_element_type=F32).astype(BF16)
        for t in range(2):
            blk = out[:, t * NB:(t + 1) * NB]
            E[2 * n + t, e, r0:r1, :] = blk
            if r0 == 0:
                R[2 * n + t, 0, 0, e, 0:CAP, :] = blk[32:48, :]
                R[2 * n + t, 0, 0, e, CAP:2 * CAP, :] = blk[64:80, :]

    def run(todo, last=True):
        for chunk, _, _ in todo:
            if chunk not in waited:
                waited.add(chunk)
                wait(fetch(chunk))
        for chunk, r0, r1 in todo:
            (layer1 if chunk[0] == 1 else layer2)(chunk, r0, r1)
        if last:
            for chunk, _, _ in todo:
                refill(slot_of[chunk])

    sends = []
    arrive = {(dx, n): [] for dx in range(2) for n in range(N8)}

    def send(parts, n0, nn, e0, ne):
        for i in parts:
            r0, dy, dc, d0 = RET[i]
            k = len(sends)
            cp = remote(E.at[pl.ds(n0, nn), pl.ds(e0, ne), pl.ds(r0, CAP), :],
                        R.at[pl.ds(n0, nn), dc, dy, pl.ds(e0, ne), pl.ds(d0, CAP), :],
                        es.at[k], er.at[k], (dy, 0, dc))
            cp.start()
            sends.append(cp)
            arrive[d0 // CAP, n0].append(cp)

    def l1(e, lo, hi, r0=0, r1=8 * CAP):
        return [((1, e, f), r0, r1) for f in range(lo, hi)]

    def l2(e, lo, hi, r0=0, r1=8 * CAP):
        return [((2, e, n), r0, r1) for n in range(lo, hi)]

    def far(k):
        fwd[k].wait_recv()
        d_s[k].start()

    run(l1(1, 0, NF, 0, NEAR), False)
    far(0)
    far(2)
    run(l2(1, 0, N4, 0, NEAR), False)
    send((0, 1, 2, 3), 0, N8, 1, 1)
    far(1)
    far(3)
    for k in range(CH):
        d_s[k].wait_recv()
    gather(3)
    run(l1(1, 0, 3, NEAR))
    run(l1(1, 3, NF, NEAR) + l1(0, 0, 3))
    run(l1(0, 3, NF))
    for n in (0, 2):
        run(l2(0, n, n + 2))
        send((4, 5, 3, 0, 1, 2), 2 * n, 4, 0, 1)
    for e in (2, 3):
        run(l1(e, 0, 4))
        run(l1(e, 4, NF))
    for n in range(N4):
        run(l2(1, n, n + 1, NEAR) + l2(2, n, n + 1) + l2(3, n, n + 1))
        for t in range(2):
            send((4, 5), 2 * n + t, 1, 1, 3)
            send((3,), 2 * n + t, 1, 2, 2)
    for n in range(N4):
        send((0, 1, 2), 2 * n, 2, 2, 2)

    gone = [remote(PX.at[n], Q.at[n], ps.at[n], pr.at[n], (0, 1, 0)) for n in range(N8)]

    outs = [pltpu.make_async_copy(PS.at[n], y_hbm.at[:, pl.ds(n * NB, NB)], ysem.at[n]) for n in range(N8)]

    def combine(dx, n):
        for cp in arrive[dx, n]:
            cp.wait_recv()
        total = jnp.zeros((TOK, NB), F32)
        for dc in range(2):
            part = jnp.dot(CM[dc, pl.ds(dx * 2 * TOK, 2 * TOK), :], R[n, dc, :, :, pl.ds(dx * CAP, CAP), :].reshape(128, NB), preferred_element_type=F32)
            g0 = GB[(dc * 2 + dx) * 2]
            g1 = GB[(dc * 2 + dx) * 2 + 1]
            g0 = jnp.concatenate([g0, g0], axis=1)
            g1 = jnp.concatenate([g1, g1], axis=1)
            total = total + (g0 * part[:TOK] + g1 * part[TOK:]).astype(BF16).astype(F32)
        return total.astype(BF16)

    def finish(n):
        gone[n].wait_recv()
        PS[n] = (PS[n].astype(F32) + Q[n].astype(F32)).astype(BF16)
        outs[n].start()

    for n in range(N8):
        PX[n] = combine(1, n)
        gone[n].start()
    for n in range(N8):
        PS[n] = combine(0, n)
        finish(n)

    for cp in metas + own_y + own_x + [own_s] + fwd + y_s + x_s + d_s + sends + gone:
        cp.wait_send()
    for cp in outs:
        cp.wait()


def solution(mesh):
    row_spec = P(('dp', 'grp', 'ing'))
    exp_spec = P(('grp', 'ing'))

    def local_fn(tokens, expert_ids, gate_vals, w_one, w_three, w_two):
        ids = expert_ids.reshape(TOK, 4).T
        gates = gate_vals.reshape(TOK, 4).T
        dma = pltpu.SemaphoreType.DMA
        anywhere = pl.BlockSpec(memory_space=pl.ANY)
        vmem = pl.BlockSpec(memory_space=pltpu.VMEM)
        return pl.pallas_call(
            kernel,
            out_shape=jax.ShapeDtypeStruct((TOK, D), BF16),
            in_specs=[vmem, vmem, anywhere, anywhere, anywhere, anywhere],
            out_specs=anywhere,
            scratch_shapes=[
                pltpu.VMEM((NS, D, 2 * FC), BF16),
                pltpu.VMEM((4, 2 * TOK, D), BF16),
                pltpu.VMEM((EL, 8 * CAP, D), BF16),
                pltpu.VMEM((3, 8 * CAP, FF), BF16),
                pltpu.VMEM((N8, EL, 8 * CAP, NB), BF16),
                pltpu.VMEM((N8, 2, 2, EL, 2 * CAP, NB), BF16),
                pltpu.VMEM((N8, TOK, NB), BF16),
                pltpu.VMEM((N8, TOK, NB), BF16),
                pltpu.VMEM((N8, TOK, NB), BF16),
                pltpu.VMEM((2, 4 * TOK, TOK), BF16),
                pltpu.VMEM((8, TOK, TOK), F32),
                pltpu.VMEM((4, 128, 256), BF16),
                pltpu.VMEM((8, 8, TOK), F32),
                dma((NS,)), dma((NS,)), dma(()),
                dma((6, CH)), dma((6, CH)), dma((1,)), dma((1,)),
                dma((7,)), dma((7,)),
                dma((64,)), dma((64,)), dma((N8,)), dma((N8,)), dma((N8,)),
            ],
            compiler_params=pltpu.CompilerParams(collective_id=0, has_side_effects=True, vmem_limit_bytes=67043328),
        )(ids, gates, tokens, w_one, w_three, w_two)

    return jax.shard_map(local_fn, mesh=mesh, in_specs=(row_spec, row_spec, row_spec, exp_spec, exp_spec, exp_spec), out_specs=row_spec, check_vma=False)
```

time: 64.8 us -> 59.9 us (0.924)
  Pallas kernels: 62.7 us -> 57.9 us
    pallas_call x1, Pallas kernels: 62.7 us -> 57.9 us  [local_fn(): pl.pallas_call(kernel, out_shape=jax.ShapeDtypeStruct((TOK, D), BF16), in...]
where the time goes in v3:
time: 59.9 us; the launch traced here: 59.8 us
  Pallas kernels  57.9 us (97%)
  local copies, waits for them, and re-layouts  1.88 us (3%)
    pallas_call x1, Pallas kernels, local_fn(): pl.pallas_call(kernel, out_shape=jax.ShapeDtypeStruct((TOK, D), BF16), in...  57.9 us
    unnamed x1, local copies, waits for them, and re-layouts  1.88 us

profile of v3, /device:TPU:0, one launch (start us, length us, event | category | flops | bytes accessed | tf_op | source)
XLA Modules:
  0.0 59.8 jit_solution(3482569291129957179)
XLA Ops:
  0.0 57.9 %shard_map.64 = bf16[128,2048]{1,0:T(8,128)(2,1)} custom-call(s32[4,128]{1,0:T(4,128)} %bitcast.6, f32[4,128]{1,0:T(4,128)} %bitcast.7, bf16[128,2048]{1,0:T(8,128)(2,1)} %tok_hbm.1, bf16[4,2048,1792]{2,1,0:T(8,128)(2,1)} %w1.1, bf16[4,2048,1792]{2,1,0:T(8,128)(2,1)} %w3.1, bf16[4,1792,2048]{2,1,0:T(8,128)(2,1)} %w2.1), custom_call_target="tpu_custom_call" | custom-call | tf_op jit(solution)/shard_map/pallas_call | solution.py:342
  57.9 1.9 %copy.8 = bf16[128,2048]{1,0:T(8,128)(2,1)} copy(bf16[128,2048]{1,0:T(8,128)(2,1)} %shard_map.64) | data formatting | bytes 1048576

commit v4 on v3

--- a/solution.py
+++ b/solution.py
@@ -31,22 +31,18 @@
 BLOCK = {(1, 0, 0): 0, (1, 0, 1): 1, (0, 0, 0): 2, (0, 0, 1): 3,
          (0, 1, 0): 4, (0, 1, 1): 5, (1, 1, 0): 6, (1, 1, 1): 7}
 NEAR = 6 * CAP
-PEERS = [(dy, dx, dc) for dy in (0, 1) for dx in (0, 1) for dc in (0, 1)][1:]
-RET = [(0, 1, 0, 0), (16, 1, 1, 0), (48, 0, 1, 0), (80, 0, 1, 16), (96, 1, 0, 16), (112, 1, 1, 16)]
-
+NEAR_PEERS = [(1, 0, 0), (0, 1, 0), (1, 0, 1), (0, 1, 1), (0, 0, 1)]
+FAR_PEERS = [(1, 1, 0), (1, 1, 1)]
+
+ORDER = (1, 0, 2, 3)
 FETCH = []
-for _e in (1, 0):
+for _e in ORDER:
     FETCH += [(1, _e, _f) for _f in range(NF)] + [(2, _e, _n) for _n in range(N4)]
-for _e in (2, 3):
-    FETCH += [(1, _e, _f) for _f in range(NF)]
-for _n in range(N4):
-    FETCH += [(2, _e, _n) for _e in (2, 3)]
-ACT = {1: 0, 2: 1, 3: 2, 0: 2}
 
 
 def kernel(ids_ref, gate_ref, tok_hbm, w1, w3, w2, y_hbm,
-           ring, T, X, act, E, R, PX, Q, PS, CM, GB, GH, META,
-           ws_a, ws_b, tsem, bs, br, ss, sr, ms, mr, es, er, ps, pr, ysem):
+           ring, T, X, act, E, R, PS, CM, GB, GH, META,
+           ws_a, ws_b, tsem, bs, br, ss, sr, ms, mr, es, er, ysem):
     g = lax.axis_index('grp')
     y = lax.axis_index('ing')
     x = g // 2
@@ -161,27 +157,24 @@
 
     lower = (lane < sub).astype(BF16)
     lane_f = lane.astype(F32)
-    for dx in range(2):
-        meta_t = jnp.transpose(jnp.concatenate([META[dx * 2], jnp.zeros((TOK - 8, TOK), F32)], axis=0))
-        ids_c = [meta_t[:, k:k + 1] for k in range(4)]
-        gate_c = [meta_t[:, 4 + k:5 + k] for k in range(4)]
-        hot_t = sum(jnp.where(ids_c[k] == lane_f, 1.0, 0.0) for k in range(4))
-        rank_t = jnp.dot(lower, hot_t.astype(BF16), preferred_element_type=F32)
-        row_of, dc_of = [], []
-        for k in range(4):
-            slot = jnp.sum(jnp.where(ids_c[k] == lane_f, rank_t, 0.0), axis=1, keepdims=True).astype(I32)
-            idi = ids_c[k].astype(I32)
-            dcr = ((idi >> 3) + c) & 1
-            dyr = ((idi >> 2) + y) & 1
-            row_of.append(dyr * 64 + (idi & 3) * CAP + slot)
-            dc_of.append(jnp.where((idi >> 4) == x, dcr, 2))
-        for dc in range(2):
-            for u in range(2):
-                sel = [dc_of[2 * m + u] == dc for m in range(2)]
-                row = jnp.where(sel[0], row_of[u], jnp.where(sel[1], row_of[2 + u], -1))
-                gate = jnp.where(sel[0], gate_c[u], jnp.where(sel[1], gate_c[2 + u], 0.0))
-                CM[dc, pl.ds((dx * 2 + u) * TOK, TOK), :] = jnp.where(row == lane, 1.0, 0.0).astype(BF16)
-                GB[(dc * 2 + dx) * 2 + u] = jnp.broadcast_to(gate, (TOK, TOK))
+    meta_t = jnp.transpose(jnp.concatenate([META[0], jnp.zeros((TOK - 8, TOK), F32)], axis=0))
+    ids_c = [meta_t[:, k:k + 1] for k in range(4)]
+    gate_c = [meta_t[:, 4 + k:5 + k] for k in range(4)]
+    hot_t = sum(jnp.where(ids_c[k] == lane_f, 1.0, 0.0) for k in range(4))
+    rank_t = jnp.dot(lower, hot_t.astype(BF16), preferred_element_type=F32)
+    row_of, grp_of = [], []
+    for k in range(4):
+        slot = jnp.sum(jnp.where(ids_c[k] == lane_f, rank_t, 0.0), axis=1, keepdims=True).astype(I32)
+        idi = ids_c[k].astype(I32)
+        row_of.append((((idi >> 2) + y) & 1) * 64 + (idi & 3) * CAP + slot)
+        grp_of.append((((idi >> 4) + x) & 1) * 2 + (((idi >> 3) + c) & 1))
+    for r in range(4):
+        for u in range(2):
+            sel = [grp_of[2 * m + u] == r for m in range(2)]
+            row = jnp.where(sel[0], row_of[u], jnp.where(sel[1], row_of[2 + u], -1))
+            gate = jnp.where(sel[0], gate_c[u], jnp.where(sel[1], gate_c[2 + u], 0.0))
+            CM[r, u * TOK:(u + 1) * TOK, :] = jnp.where(row == lane, 1.0, 0.0).astype(BF16)
+            GB[r * 2 + u] = jnp.broadcast_to(gate, (TOK, TOK))
 
     def gather(q):
         dy, dx = q // 2, q % 2
@@ -220,17 +213,16 @@
         _, e, f = chunk
         h = jnp.dot(X[e, r0:r1, :], ring[slot_of[chunk]], preferred_element_type=F32)
         h1 = h[:, :FC]
-        act[ACT[e], r0:r1, f * FC:(f + 1) * FC] = (jax.nn.silu(h1) * h[:, FC:]).astype(BF16)
+        act[e % 2, r0:r1, f * FC:(f + 1) * FC] = (jax.nn.silu(h1) * h[:, FC:]).astype(BF16)
 
     def layer2(chunk, r0, r1):
         _, e, n = chunk
-        out = jnp.dot(act[ACT[e], r0:r1, :], ring[slot_of[chunk], 0:FF, :], preferred_element_type=F32).astype(BF16)
+        out = jnp.dot(act[e % 2, r0:r1, :], ring[slot_of[chunk], 0:FF, :], preferred_element_type=F32).astype(BF16)
         for t in range(2):
             blk = out[:, t * NB:(t + 1) * NB]
             E[2 * n + t, e, r0:r1, :] = blk
             if r0 == 0:
-                R[2 * n + t, 0, 0, e, 0:CAP, :] = blk[32:48, :]
-                R[2 * n + t, 0, 0, e, CAP:2 * CAP, :] = blk[64:80, :]
+                R[2 * n + t, 0, 0, e] = blk[32:48, :]
 
     def run(todo, last=True):
         for chunk, _, _ in todo:
@@ -244,18 +236,17 @@
                 refill(slot_of[chunk])
 
     sends = []
-    arrive = {(dx, n): [] for dx in range(2) for n in range(N8)}
-
-    def send(parts, n0, nn, e0, ne):
-        for i in parts:
-            r0, dy, dc, d0 = RET[i]
+    arrive = [[] for n in range(N8)]
+
+    def send(peers, n0, nn, e):
+        for p in peers:
+            dy, dx, dc = p
             k = len(sends)
-            cp = remote(E.at[pl.ds(n0, nn), pl.ds(e0, ne), pl.ds(r0, CAP), :],
-                        R.at[pl.ds(n0, nn), dc, dy, pl.ds(e0, ne), pl.ds(d0, CAP), :],
-                        es.at[k], er.at[k], (dy, 0, dc))
+            cp = remote(E.at[pl.ds(n0, nn), e, pl.ds(BLOCK[p] * CAP, CAP), :],
+                        R.at[pl.ds(n0, nn), dx * 2 + dc, dy, e], es.at[k], er.at[k], p)
             cp.start()
             sends.append(cp)
-            arrive[d0 // CAP, n0].append(cp)
+            arrive[n0].append(cp)
 
     def l1(e, lo, hi, r0=0, r1=8 * CAP):
         return [((1, e, f), r0, r1) for f in range(lo, hi)]
@@ -267,63 +258,49 @@
         fwd[k].wait_recv()
         d_s[k].start()
 
-    run(l1(1, 0, NF, 0, NEAR), False)
+    first = ORDER[0]
+    run(l1(first, 0, NF, 0, NEAR), False)
     far(0)
     far(2)
-    run(l2(1, 0, N4, 0, NEAR), False)
-    send((0, 1, 2, 3), 0, N8, 1, 1)
+    run(l2(first, 0, N4, 0, NEAR), False)
+    send(NEAR_PEERS, 0, N8, first)
     far(1)
     far(3)
     for k in range(CH):
         d_s[k].wait_recv()
     gather(3)
-    run(l1(1, 0, 3, NEAR))
-    run(l1(1, 3, NF, NEAR) + l1(0, 0, 3))
-    run(l1(0, 3, NF))
-    for n in (0, 2):
-        run(l2(0, n, n + 2))
-        send((4, 5, 3, 0, 1, 2), 2 * n, 4, 0, 1)
-    for e in (2, 3):
-        run(l1(e, 0, 4))
-        run(l1(e, 4, NF))
+    run(l1(first, 0, 3, NEAR))
+    run(l1(first, 3, NF, NEAR))
+    run(l2(first, 0, N4, NEAR))
+    send(FAR_PEERS, 0, N8, first)
+    for e in ORDER[1:3]:
+        run(l1(e, 0, NF))
+        for n in (0, 2):
+            run(l2(e, n, n + 2))
+            send(FAR_PEERS + NEAR_PEERS, 2 * n, 4, e)
+    last = ORDER[3]
+    run(l1(last, 0, 4))
+    run(l1(last, 4, NF))
     for n in range(N4):
-        run(l2(1, n, n + 1, NEAR) + l2(2, n, n + 1) + l2(3, n, n + 1))
-        for t in range(2):
-            send((4, 5), 2 * n + t, 1, 1, 3)
-            send((3,), 2 * n + t, 1, 2, 2)
-    for n in range(N4):
-        send((0, 1, 2), 2 * n, 2, 2, 2)
-
-    gone = [remote(PX.at[n], Q.at[n], ps.at[n], pr.at[n], (0, 1, 0)) for n in range(N8)]
+        run(l2(last, n, n + 1))
+        send(FAR_PEERS + NEAR_PEERS, 2 * n, 2, last)
 
     outs = [pltpu.make_async_copy(PS.at[n], y_hbm.at[:, pl.ds(n * NB, NB)], ysem.at[n]) for n in range(N8)]
-
-    def combine(dx, n):
-        for cp in arrive[dx, n]:
+    for n in range(N8):
+        for cp in arrive[n]:
             cp.wait_recv()
         total = jnp.zeros((TOK, NB), F32)
-        for dc in range(2):
-            part = jnp.dot(CM[dc, pl.ds(dx * 2 * TOK, 2 * TOK), :], R[n, dc, :, :, pl.ds(dx * CAP, CAP), :].reshape(128, NB), preferred_element_type=F32)
-            g0 = GB[(dc * 2 + dx) * 2]
-            g1 = GB[(dc * 2 + dx) * 2 + 1]
+        for r in range(4):
+            part = jnp.dot(CM[r], R[n, r].reshape(128, NB), preferred_element_type=F32)
+            g0 = GB[r * 2]
+            g1 = GB[r * 2 + 1]
             g0 = jnp.concatenate([g0, g0], axis=1)
             g1 = jnp.concatenate([g1, g1], axis=1)
             total = total + (g0 * part[:TOK] + g1 * part[TOK:]).astype(BF16).astype(F32)
-        return total.astype(BF16)
-
-    def finish(n):
-        gone[n].wait_recv()
-        PS[n] = (PS[n].astype(F32) + Q[n].astype(F32)).astype(BF16)
+        PS[n] = total.astype(BF16)
         outs[n].start()
 
-    for n in range(N8):
-        PX[n] = combine(1, n)
-        gone[n].start()
-    for n in range(N8):
-        PS[n] = combine(0, n)
-        finish(n)
-
-    for cp in metas + own_y + own_x + [own_s] + fwd + y_s + x_s + d_s + sends + gone:
+    for cp in metas + own_y + own_x + [own_s] + fwd + y_s + x_s + d_s + sends:
         cp.wait_send()
     for cp in outs:
         cp.wait()
@@ -348,20 +325,18 @@
                 pltpu.VMEM((NS, D, 2 * FC), BF16),
                 pltpu.VMEM((4, 2 * TOK, D), BF16),
                 pltpu.VMEM((EL, 8 * CAP, D), BF16),
-                pltpu.VMEM((3, 8 * CAP, FF), BF16),
+                pltpu.VMEM((2, 8 * CAP, FF), BF16),
                 pltpu.VMEM((N8, EL, 8 * CAP, NB), BF16),
-                pltpu.VMEM((N8, 2, 2, EL, 2 * CAP, NB), BF16),
+                pltpu.VMEM((N8, 4, 2, EL, CAP, NB), BF16),
                 pltpu.VMEM((N8, TOK, NB), BF16),
-                pltpu.VMEM((N8, TOK, NB), BF16),
-                pltpu.VMEM((N8, TOK, NB), BF16),
-                pltpu.VMEM((2, 4 * TOK, TOK), BF16),
+                pltpu.VMEM((4, 2 * TOK, TOK), BF16),
                 pltpu.VMEM((8, TOK, TOK), F32),
                 pltpu.VMEM((4, 128, 256), BF16),
                 pltpu.VMEM((8, 8, TOK), F32),
                 dma((NS,)), dma((NS,)), dma(()),
                 dma((6, CH)), dma((6, CH)), dma((1,)), dma((1,)),
                 dma((7,)), dma((7,)),
-                dma((64,)), dma((64,)), dma((N8,)), dma((N8,)), dma((N8,)),
+                dma((72,)), dma((72,)), dma((N8,)),
             ],
             compiler_params=pltpu.CompilerParams(collective_id=0, has_side_effects=True, vmem_limit_bytes=67043328),
         )(ids, gates, tokens, w_one, w_three, w_two)

time: 59.9 us -> 56.5 us (0.943)
  Pallas kernels: 57.9 us -> 54.4 us
    pallas_call x1, Pallas kernels: 57.9 us -> 54.4 us  [local_fn(): pl.pallas_call(kernel, out_shape=jax.ShapeDtypeStruct((TOK, D), BF16), in...]
where the time goes in v4:
time: 56.5 us; the launch traced here: 56.3 us
  Pallas kernels  54.4 us (96%)
  local copies, waits for them, and re-layouts  1.88 us (3%)
    pallas_call x1, Pallas kernels, local_fn(): pl.pallas_call(kernel, out_shape=jax.ShapeDtypeStruct((TOK, D), BF16), in...  54.4 us
    unnamed x1, local copies, waits for them, and re-layouts  1.88 us

profile of v4, /device:TPU:0, one launch (start us, length us, event | category | flops | bytes accessed | tf_op | source)
XLA Modules:
  0.0 56.3 jit_solution(15779775528607722652)
XLA Ops:
  0.0 54.4 %shard_map.64 = bf16[128,2048]{1,0:T(8,128)(2,1)} custom-call(s32[4,128]{1,0:T(4,128)} %bitcast.6, f32[4,128]{1,0:T(4,128)} %bitcast.7, bf16[128,2048]{1,0:T(8,128)(2,1)} %tok_hbm.1, bf16[4,2048,1792]{2,1,0:T(8,128)(2,1)} %w1.1, bf16[4,2048,1792]{2,1,0:T(8,128)(2,1)} %w3.1, bf16[4,1792,2048]{2,1,0:T(8,128)(2,1)} %w2.1), custom_call_target="tpu_custom_call" | custom-call | tf_op jit(solution)/shard_map/pallas_call | solution.py:319
  54.4 1.9 %copy.8 = bf16[128,2048]{1,0:T(8,128)(2,1)} copy(bf16[128,2048]{1,0:T(8,128)(2,1)} %shard_map.64) | data formatting | bytes 1048576

commit v5 on v4

--- a/solution.py
+++ b/solution.py
@@ -26,7 +26,7 @@
 CH = 4
 CR = TOK // CH
 
-NS = 24
+NS = 23
 
 BLOCK = {(1, 0, 0): 0, (1, 0, 1): 1, (0, 0, 0): 2, (0, 0, 1): 3,
          (0, 1, 0): 4, (0, 1, 1): 5, (1, 1, 0): 6, (1, 1, 1): 7}
@@ -40,9 +40,9 @@
     FETCH += [(1, _e, _f) for _f in range(NF)] + [(2, _e, _n) for _n in range(N4)]
 
 
-def kernel(ids_ref, gate_ref, tok_hbm, w1, w3, w2, y_hbm,
-           ring, T, X, act, E, R, PS, CM, GB, GH, META,
-           ws_a, ws_b, tsem, bs, br, ss, sr, ms, mr, es, er, ysem):
+def kernel(ids_ref, gate_ref, tok_hbm, w1, w3, w2, y_ref,
+           ring, T, X, act, E, R, CM, GB, GH, META,
+           ws_a, ws_b, tsem, bs, br, ss, sr, ms, mr, es, er):
     g = lax.axis_index('grp')
     y = lax.axis_index('ing')
     x = g // 2
@@ -269,15 +269,17 @@
     for k in range(CH):
         d_s[k].wait_recv()
     gather(3)
-    run(l1(first, 0, 3, NEAR))
-    run(l1(first, 3, NF, NEAR))
+    def whole(e, cuts):
+        run(l1(e, 0, NF))
+        for lo, hi in cuts:
+            run(l2(e, lo, hi))
+            send(FAR_PEERS + NEAR_PEERS, 2 * lo, 2 * (hi - lo), e)
+
+    whole(ORDER[1], ((0, 1), (1, 2), (2, 4)))
+    run(l1(first, 0, NF, NEAR))
     run(l2(first, 0, N4, NEAR))
     send(FAR_PEERS, 0, N8, first)
-    for e in ORDER[1:3]:
-        run(l1(e, 0, NF))
-        for n in (0, 2):
-            run(l2(e, n, n + 2))
-            send(FAR_PEERS + NEAR_PEERS, 2 * n, 4, e)
+    whole(ORDER[2], ((0, 2), (2, 4)))
     last = ORDER[3]
     run(l1(last, 0, 4))
     run(l1(last, 4, NF))
@@ -285,7 +287,6 @@
         run(l2(last, n, n + 1))
         send(FAR_PEERS + NEAR_PEERS, 2 * n, 2, last)
 
-    outs = [pltpu.make_async_copy(PS.at[n], y_hbm.at[:, pl.ds(n * NB, NB)], ysem.at[n]) for n in range(N8)]
     for n in range(N8):
         for cp in arrive[n]:
             cp.wait_recv()
@@ -297,13 +298,10 @@
             g0 = jnp.concatenate([g0, g0], axis=1)
             g1 = jnp.concatenate([g1, g1], axis=1)
             total = total + (g0 * part[:TOK] + g1 * part[TOK:]).astype(BF16).astype(F32)
-        PS[n] = total.astype(BF16)
-        outs[n].start()
+        y_ref[:, n * NB:(n + 1) * NB] = total.astype(BF16)
 
     for cp in metas + own_y + own_x + [own_s] + fwd + y_s + x_s + d_s + sends:
         cp.wait_send()
-    for cp in outs:
-        cp.wait()
 
 
 def solution(mesh):
@@ -318,9 +316,9 @@
         vmem = pl.BlockSpec(memory_space=pltpu.VMEM)
         return pl.pallas_call(
             kernel,
-            out_shape=jax.ShapeDtypeStruct((TOK, D), BF16),
+            out_shape=pltpu.VMEM((TOK, D), BF16),
             in_specs=[vmem, vmem, anywhere, anywhere, anywhere, anywhere],
-            out_specs=anywhere,
+            out_specs=vmem,
             scratch_shapes=[
                 pltpu.VMEM((NS, D, 2 * FC), BF16),
                 pltpu.VMEM((4, 2 * TOK, D), BF16),
@@ -328,7 +326,6 @@
                 pltpu.VMEM((2, 8 * CAP, FF), BF16),
                 pltpu.VMEM((N8, EL, 8 * CAP, NB), BF16),
                 pltpu.VMEM((N8, 4, 2, EL, CAP, NB), BF16),
-                pltpu.VMEM((N8, TOK, NB), BF16),
                 pltpu.VMEM((4, 2 * TOK, TOK), BF16),
                 pltpu.VMEM((8, TOK, TOK), F32),
                 pltpu.VMEM((4, 128, 256), BF16),
@@ -336,9 +333,9 @@
                 dma((NS,)), dma((NS,)), dma(()),
                 dma((6, CH)), dma((6, CH)), dma((1,)), dma((1,)),
                 dma((7,)), dma((7,)),
-                dma((72,)), dma((72,)), dma((N8,)),
+                dma((72,)), dma((72,)),
             ],
-            compiler_params=pltpu.CompilerParams(collective_id=0, has_side_effects=True, vmem_limit_bytes=67043328),
+            compiler_params=pltpu.CompilerParams(collective_id=0, has_side_effects=True, vmem_limit_bytes=65000000),
         )(ids, gates, tokens, w_one, w_three, w_two)
 
     return jax.shard_map(local_fn, mesh=mesh, in_specs=(row_spec, row_spec, row_spec, exp_spec, exp_spec, exp_spec), out_specs=row_spec, check_vma=False)

time: 56.5 us -> 53.6 us (0.949)
  Pallas kernels: 54.4 us -> 52.6 us
  local copies, waits for them, and re-layouts: 1.88 us -> 0.8 us
    pallas_call x1, Pallas kernels: 54.4 us -> 52.6 us  [local_fn(): pl.pallas_call(kernel, out_shape=pltpu.VMEM((TOK, D), BF16), in_specs=[vm...]
    unnamed x1, local copies, waits for them, and re-layouts: 1.88 us -> 0.8 us
where the time goes in v5:
time: 53.6 us; the launch traced here: 53.4 us
  Pallas kernels  52.6 us (98%)
  local copies, waits for them, and re-layouts  0.8 us (1%)
    pallas_call x1, Pallas kernels, local_fn(): pl.pallas_call(kernel, out_shape=pltpu.VMEM((TOK, D), BF16), in_specs=[vm...  52.6 us

profile of v5, /device:TPU:0, one launch (start us, length us, event | category | flops | bytes accessed | tf_op | source)
XLA Modules:
  0.0 53.4 jit_solution(17831416632050261681)
XLA Ops:
  0.0 52.6 %shard_map.64 = bf16[128,2048]{1,0:T(8,128)(2,1)S(1)} custom-call(s32[4,128]{1,0:T(4,128)} %bitcast.6, f32[4,128]{1,0:T(4,128)} %bitcast.7, bf16[128,2048]{1,0:T(8,128)(2,1)} %tok_hbm.1, bf16[4,2048,1792]{2,1,0:T(8,128)(2,1)} %w1.1, bf16[4,2048,1792]{2,1,0:T(8,128)(2,1)} %w3.1, bf16[4,1792,2048]{2,1,0:T(8,128)(2,1)} %w2.1), custom_call_target="tpu_custom_call" | custom-call | tf_op jit(solution)/shard_map/pallas_call | solution.py:317
  52.6 0.8 %copy.8 = bf16[128,2048]{1,0:T(8,128)(2,1)} copy(bf16[128,2048]{1,0:T(8,128)(2,1)S(1)} %shard_map.64) | data formatting | bytes 1048576

commit v6 on v5

--- a/solution.py
+++ b/solution.py
@@ -40,9 +40,9 @@
     FETCH += [(1, _e, _f) for _f in range(NF)] + [(2, _e, _n) for _n in range(N4)]
 
 
-def kernel(ids_ref, gate_ref, tok_hbm, w1, w3, w2, y_ref,
-           ring, T, X, act, E, R, CM, GB, GH, META,
-           ws_a, ws_b, tsem, bs, br, ss, sr, ms, mr, es, er):
+def kernel(ids_hbm, gate_hbm, tok_hbm, w1, w3, w2, y_ref,
+           ids_ref, gate_ref, ring, T, X, act, E, R, CM, GB, GH, META,
+           ws_a, ws_b, tsem, isem, bs, br, ss, sr, ms, mr, es, er):
     g = lax.axis_index('grp')
     y = lax.axis_index('ing')
     x = g // 2
@@ -71,6 +71,9 @@
             cp.wait()
 
     own = pltpu.make_async_copy(tok_hbm, T.at[0, pl.ds(0, TOK), :], tsem)
+    small = [pltpu.make_async_copy(ids_hbm, ids_ref, isem.at[0]), pltpu.make_async_copy(gate_hbm, gate_ref, isem.at[1])]
+    for cp in small:
+        cp.start()
     own.start()
     slot_of = {}
     queue = list(FETCH)
@@ -88,12 +91,13 @@
     for i in range(NS):
         refill(i)
 
-    META[0] = jnp.concatenate([ids_ref[...].astype(F32), gate_ref[...]], axis=0)
-
     barrier = pltpu.get_barrier_semaphore()
     direct = [(0, 0, 1), (0, 1, 0), (1, 0, 0), (1, 0, 1)]
     for p in direct:
         pl.semaphore_signal(barrier, inc=1, device_id=peer(*p), device_id_type=MESH)
+    for cp in small:
+        cp.wait()
+    META[0] = jnp.concatenate([ids_ref[...].astype(F32), gate_ref[...]], axis=0)
     pl.semaphore_wait(barrier, len(direct))
 
     metas = [remote(META.at[i], META.at[j], ms.at[k], mr.at[k], to) for k, (i, j, to) in enumerate([
@@ -220,9 +224,9 @@
         out = jnp.dot(act[e % 2, r0:r1, :], ring[slot_of[chunk], 0:FF, :], preferred_element_type=F32).astype(BF16)
         for t in range(2):
             blk = out[:, t * NB:(t + 1) * NB]
-            E[2 * n + t, e, r0:r1, :] = blk
+            E[e, r0 // CAP:r1 // CAP, 2 * n + t] = blk.reshape((r1 - r0) // CAP, CAP, NB)
             if r0 == 0:
-                R[2 * n + t, 0, 0, e] = blk[32:48, :]
+                R[0, 0, e, 2 * n + t] = blk[32:48, :]
 
     def run(todo, last=True):
         for chunk, _, _ in todo:
@@ -242,8 +246,7 @@
         for p in peers:
             dy, dx, dc = p
             k = len(sends)
-            cp = remote(E.at[pl.ds(n0, nn), e, pl.ds(BLOCK[p] * CAP, CAP), :],
-                        R.at[pl.ds(n0, nn), dx * 2 + dc, dy, e], es.at[k], er.at[k], p)
+            cp = remote(E.at[e, BLOCK[p], pl.ds(n0, nn)], R.at[dx * 2 + dc, dy, e, pl.ds(n0, nn)], es.at[k], er.at[k], p)
             cp.start()
             sends.append(cp)
             arrive[n0].append(cp)
@@ -262,8 +265,9 @@
     run(l1(first, 0, NF, 0, NEAR), False)
     far(0)
     far(2)
-    run(l2(first, 0, N4, 0, NEAR), False)
-    send(NEAR_PEERS, 0, N8, first)
+    for n in (0, 2):
+        run(l2(first, n, n + 2, 0, NEAR), False)
+        send(NEAR_PEERS, 2 * n, 4, first)
     far(1)
     far(3)
     for k in range(CH):
@@ -283,16 +287,16 @@
     last = ORDER[3]
     run(l1(last, 0, 4))
     run(l1(last, 4, NF))
-    for n in range(N4):
-        run(l2(last, n, n + 1))
-        send(FAR_PEERS + NEAR_PEERS, 2 * n, 2, last)
+    for lo, hi in ((0, 2), (2, 3), (3, 4)):
+        run(l2(last, lo, hi))
+        send(NEAR_PEERS + FAR_PEERS, 2 * lo, 2 * (hi - lo), last)
 
     for n in range(N8):
         for cp in arrive[n]:
             cp.wait_recv()
         total = jnp.zeros((TOK, NB), F32)
         for r in range(4):
-            part = jnp.dot(CM[r], R[n, r].reshape(128, NB), preferred_element_type=F32)
+            part = jnp.dot(CM[r], R[r, :, :, n].reshape(128, NB), preferred_element_type=F32)
             g0 = GB[r * 2]
             g1 = GB[r * 2 + 1]
             g0 = jnp.concatenate([g0, g0], axis=1)
@@ -317,20 +321,21 @@
         return pl.pallas_call(
             kernel,
             out_shape=pltpu.VMEM((TOK, D), BF16),
-            in_specs=[vmem, vmem, anywhere, anywhere, anywhere, anywhere],
+            in_specs=[anywhere, anywhere, anywhere, anywhere, anywhere, anywhere],
             out_specs=vmem,
             scratch_shapes=[
+                pltpu.VMEM((4, TOK), I32), pltpu.VMEM((4, TOK), F32),
                 pltpu.VMEM((NS, D, 2 * FC), BF16),
                 pltpu.VMEM((4, 2 * TOK, D), BF16),
                 pltpu.VMEM((EL, 8 * CAP, D), BF16),
                 pltpu.VMEM((2, 8 * CAP, FF), BF16),
-                pltpu.VMEM((N8, EL, 8 * CAP, NB), BF16),
-                pltpu.VMEM((N8, 4, 2, EL, CAP, NB), BF16),
+                pltpu.VMEM((EL, 8, N8, CAP, NB), BF16),
+                pltpu.VMEM((4, 2, EL, N8, CAP, NB), BF16),
                 pltpu.VMEM((4, 2 * TOK, TOK), BF16),
                 pltpu.VMEM((8, TOK, TOK), F32),
                 pltpu.VMEM((4, 128, 256), BF16),
                 pltpu.VMEM((8, 8, TOK), F32),
-                dma((NS,)), dma((NS,)), dma(()),
+                dma((NS,)), dma((NS,)), dma(()), dma((2,)),
                 dma((6, CH)), dma((6, CH)), dma((1,)), dma((1,)),
                 dma((7,)), dma((7,)),
                 dma((72,)), dma((72,)),

time: 53.6 us -> 52.6 us (0.981)
  Pallas kernels: 52.6 us -> 51.7 us
    pallas_call x1, Pallas kernels: 52.6 us -> 51.7 us  [local_fn(): pl.pallas_call(kernel, out_shape=pltpu.VMEM((TOK, D), BF16), in_specs=[an...]
where the time goes in v6:
time: 52.6 us; the launch traced here: 52.5 us
  Pallas kernels  51.7 us (98%)
  local copies, waits for them, and re-layouts  0.8 us (2%)
    pallas_call x1, Pallas kernels, local_fn(): pl.pallas_call(kernel, out_shape=pltpu.VMEM((TOK, D), BF16), in_specs=[an...  51.7 us

profile of v6, /device:TPU:0, one launch (start us, length us, event | category | flops | bytes accessed | tf_op | source)
XLA Modules:
  0.0 52.5 jit_solution(8624139777426100311)
XLA Ops:
  0.0 51.7 %shard_map.64 = bf16[128,2048]{1,0:T(8,128)(2,1)S(1)} custom-call(s32[4,128]{1,0:T(4,128)} %bitcast.6, f32[4,128]{1,0:T(4,128)} %bitcast.7, bf16[128,2048]{1,0:T(8,128)(2,1)} %tok_hbm.1, bf16[4,2048,1792]{2,1,0:T(8,128)(2,1)} %w1.1, bf16[4,2048,1792]{2,1,0:T(8,128)(2,1)} %w3.1, bf16[4,1792,2048]{2,1,0:T(8,128)(2,1)} %w2.1), custom_call_target="tpu_custom_call" | custom-call | tf_op jit(solution)/shard_map/pallas_call | solution.py:321
  51.7 0.8 %copy.8 = bf16[128,2048]{1,0:T(8,128)(2,1)} copy(bf16[128,2048]{1,0:T(8,128)(2,1)S(1)} %shard_map.64) | data formatting | bytes 1048576

commit v7 on v6

--- a/solution.py
+++ b/solution.py
@@ -54,6 +54,11 @@
     def remote(src, dst, s, r, to):
         return pltpu.make_async_remote_copy(src_ref=src, dst_ref=dst, send_sem=s, recv_sem=r, device_id=peer(*to), device_id_type=MESH)
 
+    barrier = pltpu.get_barrier_semaphore()
+    direct = [(0, 0, 1), (0, 1, 0), (1, 0, 0), (1, 0, 1)]
+    for p in direct:
+        pl.semaphore_signal(barrier, inc=1, device_id=peer(*p), device_id_type=MESH)
+
     def w13(e, f, slot):
         col = pl.ds(pl.multiple_of(f * FC, FC), FC)
         return (pltpu.make_async_copy(w1.at[e, :, col], ring.at[slot, :, pl.ds(0, FC)], ws_a.at[slot]),
@@ -88,13 +93,6 @@
             slot_of[chunk] = slot
             start(fetch(chunk))
 
-    for i in range(NS):
-        refill(i)
-
-    barrier = pltpu.get_barrier_semaphore()
-    direct = [(0, 0, 1), (0, 1, 0), (1, 0, 0), (1, 0, 1)]
-    for p in direct:
-        pl.semaphore_signal(barrier, inc=1, device_id=peer(*p), device_id_type=MESH)
     for cp in small:
         cp.wait()
     META[0] = jnp.concatenate([ids_ref[...].astype(F32), gate_ref[...]], axis=0)
@@ -132,6 +130,9 @@
         own_y[k].start()
         own_x[k].start()
     own_s.start()
+
+    for i in range(NS):
+        refill(i)
 
     metas[4].wait_recv()
     metas[6].start()

time: 52.6 us -> 52.6 us (level)
  no operation moved by 1% of the time
where the time goes in v7:
time: 52.6 us; the launch traced here: 52.4 us
  Pallas kernels  51.6 us (98%)
  local copies, waits for them, and re-layouts  0.8 us (2%)
    pallas_call x1, Pallas kernels, local_fn(): pl.pallas_call(kernel, out_shape=pltpu.VMEM((TOK, D), BF16), in_specs=[an...  51.6 us

profile of v7, /device:TPU:0, one launch (start us, length us, event | category | flops | bytes accessed | tf_op | source)
XLA Modules:
  0.0 52.4 jit_solution(9321855959906881300)
XLA Ops:
  0.0 51.6 %shard_map.64 = bf16[128,2048]{1,0:T(8,128)(2,1)S(1)} custom-call(s32[4,128]{1,0:T(4,128)} %bitcast.6, f32[4,128]{1,0:T(4,128)} %bitcast.7, bf16[128,2048]{1,0:T(8,128)(2,1)} %tok_hbm.1, bf16[4,2048,1792]{2,1,0:T(8,128)(2,1)} %w1.1, bf16[4,2048,1792]{2,1,0:T(8,128)(2,1)} %w3.1, bf16[4,1792,2048]{2,1,0:T(8,128)(2,1)} %w2.1), custom_call_target="tpu_custom_call" | custom-call | tf_op jit(solution)/shard_map/pallas_call | solution.py:322
  51.7 0.8 %copy.8 = bf16[128,2048]{1,0:T(8,128)(2,1)} copy(bf16[128,2048]{1,0:T(8,128)(2,1)S(1)} %shard_map.64) | data formatting | bytes 1048576
